TPU v7x, 32 devices: a whole 2x2x4 slice. The times are simulated.
32 devices in a mesh: px: 8 (over z, y), py: 4 (over x, core).
Axes of the slice: x: 2, y: 2, z: 4, core: 2. Of those that a mesh axis runs over, the one named last changes fastest.
Arguments:
- field: bfloat16 [1, 32, 128, 128, 256], P(None, None, 'px', 'py'), may hold values from -6 to 6
- spectral_weight: bfloat16 [2, 32, 32, 32, 64, 64], P(None, None, 'px', 'py'), may hold values from -72 to 72
- point_weight: bfloat16 [32, 32], replicated, may hold values from -1 to 1
- point_bias: float32 [32], replicated, may hold values from -3 to 3
Outputs:
- layer_out: bfloat16 [1, 32, 128, 128, 256], P(None, None, 'px', 'py')
All inputs are finite; a program needn't handle non-finite values.
Results may differ from a plain program's by a relative error of at most 0.0085.
Values may be sent and summed in bfloat16 or wider, within the bound.
A program may use at most 192 MiB of HBM per device.

v0:
```python
from functools import partial
import math
import jax
import jax.numpy as jnp
from jax import lax
from jax.sharding import PartitionSpec as P

MX = 64
MY = 64
MZ = 32


def contract(form, left, right):
    return jnp.einsum(
        form, left, right, precision=lax.Precision.HIGHEST, preferred_element_type=jnp.float32
    )


def angle_table(length, count, signed):
    position = jnp.arange(length, dtype=jnp.int32)
    number = jnp.arange(count, dtype=jnp.int32)
    if signed:
        number = jnp.where(number < count // 2, number, number - count)
    product = position[:, None] * number[None, :] % length
    return 2.0 * math.pi / length * product.astype(jnp.float32)


def forward_x(piece, keep_count, cos_x, sin_x):
    real_part = piece[0]
    imag_part = piece[1]
    out_real = contract("ix,bcxm->bcim", cos_x, real_part) + contract(
        "ix,bcxm->bcim", sin_x, imag_part
    )
    out_imag = contract("ix,bcxm->bcim", cos_x, imag_part) - contract(
        "ix,bcxm->bcim", sin_x, real_part
    )
    return jnp.stack([out_real, out_imag], axis=0)


def inverse_z(piece, table):
    return contract("pbcxky,pkz->bcxyz", piece, table)


def body(field, spectral_weight, point_weight, point_bias):
    batch, channels, rows_x, rows_y, depth = field.shape
    grid_x = rows_x * lax.axis_size("px")
    grid_y = rows_y * lax.axis_size("py")
    theta_x = angle_table(grid_x, MX, True)
    theta_y = angle_table(grid_y, MY, True)
    wide = field.astype(jnp.float32)
    count = MZ
    theta_z = angle_table(depth, count, False)
    z_real = contract("bcxyz,zk->bcxky", wide, jnp.cos(theta_z))
    z_imag = contract("bcxyz,zk->bcxky", wide, -jnp.sin(theta_z))
    along_z = jnp.stack([z_real, z_imag], axis=0).reshape(
        2, batch, channels, rows_x, count * rows_y
    )
    step_x = partial(
        forward_x, keep_count=MZ * rows_y, cos_x=jnp.cos(theta_x).T, sin_x=jnp.sin(theta_x).T
    )
    along_x = step_x(lax.all_to_all(along_z, "px", split_axis=2, concat_axis=3, tiled=True))
    shape = along_x.shape
    along_x = along_x.reshape(shape[0], shape[1], shape[2], shape[3], MZ, rows_y)
    moved = lax.all_to_all(along_x, "py", split_axis=4, concat_axis=5, tiled=True)
    cos_y = jnp.cos(theta_y)
    sin_y = jnp.sin(theta_y)
    spec_real = contract("bciky,yj->bcikj", moved[0], cos_y) + contract(
        "bciky,yj->bcikj", moved[1], sin_y
    )
    spec_imag = contract("bciky,yj->bcikj", moved[1], cos_y) - contract(
        "bciky,yj->bcikj", moved[0], sin_y
    )
    spectrum = jnp.stack([spec_real, spec_imag], axis=0).astype(jnp.bfloat16)
    gathered = lax.all_gather(spectrum, "px", axis=2, tiled=True)
    in_real = gathered[0].astype(jnp.float32)
    in_imag = gathered[1].astype(jnp.float32)
    weight_real = spectral_weight[0].astype(jnp.float32)
    weight_imag = spectral_weight[1].astype(jnp.float32)
    mixed_real = contract("bcikj,cokij->boikj", in_real, weight_real) - contract(
        "bcikj,cokij->boikj", in_imag, weight_imag
    )
    mixed_imag = contract("bcikj,cokij->boikj", in_real, weight_imag) + contract(
        "bcikj,cokij->boikj", in_imag, weight_real
    )
    cos_yt = jnp.cos(theta_y).T
    sin_yt = jnp.sin(theta_y).T
    back_real = contract("boikj,jy->boiky", mixed_real, cos_yt) - contract(
        "boikj,jy->boiky", mixed_imag, sin_yt
    )
    back_imag = contract("boikj,jy->boiky", mixed_real, sin_yt) + contract(
        "boikj,jy->boiky", mixed_imag, cos_yt
    )
    returned = lax.all_to_all(
        jnp.stack([back_real, back_imag], axis=0), "py", split_axis=5, concat_axis=4, tiled=True
    )
    cos_xt = jnp.cos(theta_x)
    sin_xt = jnp.sin(theta_x)
    out_real = contract("xi,boiky->boxky", cos_xt, returned[0]) - contract(
        "xi,boiky->boxky", sin_xt, returned[1]
    )
    out_imag = contract("xi,boiky->boxky", sin_xt, returned[0]) + contract(
        "xi,boiky->boxky", cos_xt, returned[1]
    )
    planes = jnp.stack([out_real, out_imag], axis=0)
    theta_back = angle_table(depth, MZ, False).T
    factor = jnp.where(jnp.arange(MZ) == 0, 1.0, 2.0).astype(jnp.float32) / float(
        grid_x * grid_y * depth
    )
    table_back = jnp.stack(
        [factor[:, None] * jnp.cos(theta_back), -factor[:, None] * jnp.sin(theta_back)], axis=0
    )
    spectral = inverse_z(
        lax.all_to_all(planes, "px", split_axis=3, concat_axis=2, tiled=True), table=table_back
    )
    pointwise = jnp.einsum(
        "oc,bcxyz->boxyz", point_weight, field, preferred_element_type=jnp.float32
    )
    pointwise = pointwise + point_bias[None, :, None, None, None]
    return jax.nn.gelu(spectral + pointwise, approximate=False).astype(jnp.bfloat16)


def solution(mesh):
    placed = (P(None, None, "px", "py", None), P(None, None, "px", "py", None, None), P(), P())
    return jax.shard_map(
        body, mesh=mesh, in_specs=placed, out_specs=P(None, None, "px", "py", None), check_vma=False
    )
```

profile of v0, /device:TPU:0, one launch (start us, length us, event | category | flops | bytes accessed | tf_op | source)
XLA Modules:
  0.0 746.2 jit_solution(797422356262062606)
XLA Ops:
  6.5 24.2 %convolution_bitcast_fusion.1 = f32[1,32,16,32,32]{4,3,2,1,0:T(8,128)} fusion(bf16[1,32,16,32,256]{4,3,2,1,0:T(8,128)(2,1)} %param.4), kind=kOutput, calls=%fused_computation.41 | convolution fusion | flops 1610727424 | bytes 10485760 | tf_op jit(solution)/shard_map/bcxyz,zk->bcxky/dot_general | solution.py:14
  30.8 21.1 %convolution_bitcast_fusion = f32[1,32,16,32,32]{4,3,2,1,0:T(8,128)} fusion(bf16[1,32,16,32,256]{4,3,2,1,0:T(8,128)(2,1)S(1)} %copy-done.2), kind=kOutput, calls=%fused_computation.40 | convolution fusion | flops 1610735616 | bytes 10485760 | tf_op jit(solution)/shard_map/bcxyz,zk->bcxky/dot_general | solution.py:14
  51.9 6.6 stack.50
  58.6 7.9 %stack.51 = f32[1,1,32,16,1024]{4,3,2,1,0:T(8,128)} reshape(f32[1,32,16,32,32]{4,3,2,1,0:T(8,128)} %convolution_bitcast_fusion) | data formatting | bytes 4194304 | tf_op jit(solution)/shard_map/stack | solution.py:55
  66.5 4.4 pad_maximum_fusion
  70.8 7.3 all-to-all-start
  78.2 93.2 %all-to-all-done = f32[2,1,32,16,1024]{4,3,1,0,2:T(8,128)} async-done(((f32[2,1,32,16,1024]{4,3,1,0,2:T(8,128)}), f32[2,1,32,16,1024]{4,3,1,0,2:T(8,128)}, u32[]{:S(2)}, u32[]{:S(2)}) %all-to-all-start) | async-done | bytes 4194336 | tf_op jit(solution)/shard_map/all_to_all | solution.py:61
  171.4 2.5 copy.147
  173.9 0.6 fusion.179
  174.5 1.5 fusion.63
  176.1 1.5 fusion.65
  177.6 1.6 fusion.20
  179.2 2.6 fusion.21
  181.7 1.8 copy.50
  183.6 2.0 copy.51
  185.5 4.4 copy_bitcast_fusion.2
  189.9 4.5 reshape.325
  194.4 28.9 %all_to_all.60 = f32[4,1,131072]{2,1,0:T(1,128)} all-to-all(f32[4,1,131072]{2,1,0:T(1,128)S(1)} %reshape.325), channel_id=1, replica_groups=mesh['px'=8,'py'=4] {'py'}, dimensions={0} | all-to-all | bytes 4194304 | tf_op jit(solution)/shard_map/all_to_all | solution.py:64
  223.3 0.5 broadcast.331
  223.9 7.7 %reduce.8 = f32[4,131072]{1,0:T(4,128)S(1)} reduce(f32[4,1,131072]{2,1,0:T(1,128)} %all_to_all.60, f32[]{:T(128)} %broadcast.331), dimensions={1}, to_apply=%all_to_all.47.reduce_sub_computation | reduce | bytes 4194308 | tf_op jit(solution)/shard_map/all_to_all | solution.py:64
  231.6 4.0 reshape.326
  235.6 2.8 copy.146
  238.4 2.0 fusion.178
  240.4 0.6 copy.54
  241.0 2.2 copy.55
  243.3 1.2 fusion.57
  244.4 1.2 fusion.59
  245.6 1.3 fusion.24
  247.0 1.2 fusion.25
  248.2 1.2 pad_maximum_fusion.4
  249.4 122.7 %all-gather.2.cloned.1.call-done = bf16[2,1,32,64,8,64]{5,4,3,2,1,0:T(8,128)(2,1)} async-done(((bf16[2,1,4,64,8,64]{5,4,3,2,1,0:T(8,128)(2,1)}), bf16[2,1,32,64,8,64]{5,4,3,2,1,0:T(8,128)(2,1)}) %all-gather.2.cloned.1.call-update) | async-done | bytes 4194320 | tf_op jit(solution)/shard_map/all_gather | solution.py:74
  372.1 11.7 %fusion.16 = (f32[64,8,64,32]{2,1,0,3:T(8,128)}, f32[64,8,64,32]{2,1,0,3:T(8,128)}) fusion(bf16[2,1,32,64,8,64]{5,4,3,2,1,0:T(8,128)(2,1)} %all-gather.2.cloned.1.call-done), kind=kLoop, calls=%fused_computation.32 | loop fusion | flops 2097152 | bytes 12582912
  383.8 8.4 %copy.107 = f32[64,8,64,32]{2,0,1,3:T(8,128)} copy(f32[64,8,64,32]{2,1,0,3:T(8,128)} %get-tuple-element.11) | data formatting | bytes 8388608
  392.2 5.0 copy.106
  397.2 23.1 %fusion.3 = (f32[64,8,64,4]{2,0,1,3:T(8,128)S(1)}, f32[64,8,64,4]{2,0,1,3:T(8,128)S(1)}, f32[64,8,64,4]{2,0,1,3:T(8,128)}, f32[64,8,64,4]{2,0,1,3:T(8,128)S(1)}) fusion(f32[64,8,64,32]{2,0,1,3:T(8,128)} %copy.106, bf16[2,32,4,8,64,64]{5,4,3,2,1,0:T(8,128)(2,1)} %param.5, f32[64,8,64,32]{2,0,1,3:T(8,128)} %copy.107), kind=kLoop, calls=%fused_computation.7 | loop fusion | flops 41418752 | bytes 27262976
  420.3 3.8 fusion.28
  424.1 3.8 fusion.30
  427.9 2.4 fusion.19
  430.3 2.4 fusion.18
  432.7 0.1 pad_maximum_fusion.3
  432.8 4.7 copy.58
  437.5 4.5 reshape.327
  442.0 28.9 %all_to_all.61 = f32[4,1,131072]{2,1,0:T(1,128)} all-to-all(f32[4,1,131072]{2,1,0:T(1,128)S(1)} %reshape.327), channel_id=1, replica_groups=mesh['px'=8,'py'=4] {'py'}, dimensions={0} | all-to-all | bytes 4194304 | tf_op jit(solution)/shard_map/all_to_all | solution.py:93
  470.9 7.7 %reduce.9 = f32[4,131072]{1,0:T(4,128)S(1)} reduce(f32[4,1,131072]{2,1,0:T(1,128)} %all_to_all.61, f32[]{:T(128)} %broadcast.331), dimensions={1}, to_apply=%all_to_all.50.reduce_sub_computation | reduce | bytes 4194308 | tf_op jit(solution)/shard_map/all_to_all | solution.py:93
  478.6 4.0 reshape.328
  482.6 4.6 copy.59
  487.2 0.8 fusion.177
  488.0 0.2 copy.60
  488.3 2.2 fusion.45
  490.5 2.1 fusion.53
  492.6 0.2 copy.61
  492.8 2.0 subtract_bitcast_fusion
  494.8 2.0 add_bitcast_fusion
  496.9 2.8 pad_maximum_fusion.2
  499.7 14.4 %copy.62 = f32[2,1,4,128,32,32]{5,4,2,1,0,3:T(8,128)} copy(f32[2,1,4,128,32,32]{3,5,4,2,1,0:T(8,128)} %pad_maximum_fusion.2) | data formatting | bytes 8388608 | tf_op jit(solution)/shard_map/stack | solution.py:104
  514.0 12.8 %reshape.329 = f32[8,1,131072]{2,1,0:T(1,128)} reshape(f32[128,2,1,4,32,32]{5,4,3,2,1,0:T(8,128)} %bitcast.215) | data formatting | bytes 8388608
  526.9 4.8 all-to-all-start.3
  531.8 14.2 %fusion.14 = f32[16,32,256,32]{2,3,1,0:T(8,128)} fusion(bf16[32,16,32,256]{3,2,1,0:T(8,128)(2,1)} %bitcast.214, bf16[32,32]{1,0:T(8,128)(2,1)S(1)} %copy-done), kind=kOutput, calls=%fused_computation.29 | convolution fusion | flops 268435456 | bytes 25167872 | tf_op jit(solution)/shard_map/oc,bcxyz->boxyz/dot_general | solution.py:115
  546.0 78.7 %all-to-all-done.3 = f32[8,1,131072]{2,1,0:T(1,128)} async-done(((f32[8,1,131072]{2,1,0:T(1,128)}), f32[8,1,131072]{2,1,0:T(1,128)}, u32[]{:S(2)}, u32[]{:S(2)}) %all-to-all-start.3) | async-done | bytes 4194336 | tf_op jit(solution)/shard_map/all_to_all | solution.py:113
  624.7 14.9 %reduce.10 = f32[8,131072]{1,0:T(8,128)} reduce(f32[8,1,131072]{2,1,0:T(1,128)} %all-to-all-done.3, f32[]{:T(128)} %broadcast.331), dimensions={1}, to_apply=%all_to_all.53.reduce_sub_computation | reduce | bytes 8388612 | tf_op jit(solution)/shard_map/all_to_all | solution.py:113
  639.6 13.3 %reshape.330 = f32[128,2,1,4,32,32]{5,4,3,2,1,0:T(8,128)} reshape(f32[8,131072]{1,0:T(8,128)} %reduce.10) | data formatting | bytes 8388608
  653.0 11.8 %copy.63 = f32[2,1,4,128,32,32]{5,4,3,2,0,1:T(8,128)} copy(f32[2,1,4,128,32,32]{5,4,2,1,0,3:T(8,128)} %bitcast.216) | data formatting | bytes 8388608 | tf_op jit(solution)/shard_map/all_to_all | solution.py:113
  664.7 16.4 %copy.64 = f32[2,1,8,4,16,32,32]{5,6,0,4,3,2,1:T(8,128)} copy(f32[2,1,8,4,16,32,32]{6,5,4,2,3,0,1:T(8,128)} %bitcast.217) | data formatting | bytes 8388608 | tf_op jit(solution)/shard_map/all_to_all | solution.py:113
  681.2 57.7 %fusion.6 = bf16[1,32,16,32,256]{4,3,2,1,0:T(8,128)(2,1)} fusion(f32[16,32,256,32]{2,3,1,0:T(8,128)} %fusion.14, f32[2,32,16,32,32]{3,4,0,2,1:T(8,128)} %bitcast.227, f32[32]{0:T(128)S(1)} %copy-done.4, f32[1,32,256]{2,1,0:T(8,128)S(1)} %get-tuple-element.19, f32[1,32,256]{2,1,0:T(8,128)S(1)} %get-tuple-element.20), kind=kOutput, calls=%fused_computation.11 | convolution fusion | flops 3502260224 | bytes 29425792 | tf_op jit(solution)/shard_map/pbcxky,pkz->bcxyz/dot_general | solution.py:14
  (16 shorter events, 0.2 us)
Async XLA Ops:
  6.5 525.3 %copy-start = (bf16[32,32]{1,0:T(8,128)(2,1)S(1)}, bf16[32,32]{1,0:T(8,128)(2,1)}, u32[]{:S(2)}) copy-start(bf16[32,32]{1,0:T(8,128)(2,1)} %param.6) | copy-start | bytes 6148
  6.5 24.2 %copy-start.2 = (bf16[1,32,16,32,256]{4,3,2,1,0:T(8,128)(2,1)S(1)}, bf16[1,32,16,32,256]{4,3,2,1,0:T(8,128)(2,1)}, u32[]{:S(2)}) copy-start(bf16[1,32,16,32,256]{4,3,2,1,0:T(8,128)(2,1)} %param.4) | copy-start | bytes 25165828
  70.8 100.6 %all-to-all-start = ((f32[2,1,32,16,1024]{4,3,1,0,2:T(8,128)}), f32[2,1,32,16,1024]{4,3,1,0,2:T(8,128)}, u32[]{:S(2)}, u32[]{:S(2)}) async-start(f32[2,1,32,16,1024]{4,3,1,0,2:T(8,128)} %pad_maximum_fusion), calls=%async_computation | async-start | bytes 8388608 | tf_op jit(solution)/shard_map/all_to_all | solution.py:61
  78.2 294.0 %all-gather.2.cloned.1.call-start = ((), (), s32[]{:S(2)}) async-start(), calls=%async_computation.4 | async-start | bytes 9437184 | tf_op jit(solution)/shard_map/all_gather | solution.py:74
  383.8 8.4 %copy-start.3 = (f32[64,8,64,32]{2,1,0,3:T(8,128)S(1)}, f32[64,8,64,32]{2,1,0,3:T(8,128)}, u32[]{:S(2)}) copy-start(f32[64,8,64,32]{2,1,0,3:T(8,128)} %get-tuple-element.12) | copy-start | bytes 12582916
  526.9 97.8 %all-to-all-start.3 = ((f32[8,1,131072]{2,1,0:T(1,128)}), f32[8,1,131072]{2,1,0:T(1,128)}, u32[]{:S(2)}, u32[]{:S(2)}) async-start(f32[8,1,131072]{2,1,0:T(1,128)} %reshape.329), calls=%async_computation.3 | async-start | bytes 8388608 | tf_op jit(solution)/shard_map/all_to_all | solution.py:113
  664.7 16.4 %copy-start.4 = (f32[32]{0:T(128)S(1)}, f32[32]{0:T(128)}, u32[]{:S(2)}) copy-start(f32[32]{0:T(128)} %param.7) | copy-start | bytes 388
  681.2 57.7 %copy-start.1 = (bf16[32,32]{1,0:T(8,128)(2,1)S(1)}, bf16[32,32]{1,0:T(8,128)(2,1)}, u32[]{:S(2)}) copy-start(bf16[32,32]{1,0:T(8,128)(2,1)} %param.6) | copy-start | bytes 6148
Sparse Core Ops, SparseCore 0:
  249.5 122.5 all-gather.1
where the time goes:
time: 756 us; the launch traced here: 746 us
  waiting for transfers between devices  295 us (39%)
  matrix products  150 us (20%)
  local copies, waits for them, and re-layouts  139 us (18%)
  other arithmetic  78.1 us (10%)
  blocking collectives  57.8 us (8%)
  between operations  14.2 us (2%)
  starting transfers between devices  12.1 us (2%)
    dot_general x19, matrix products, contract(): jnp.einsum(form, left, right, precision=lax.Precision.HIGHEST, preferred_...  136 us
    all_gather x1, waiting for transfers between devices, body(): gathered = lax.all_gather(spectrum, 'px', axis=2, tiled=True)  123 us
    all_to_all x1, waiting for transfers between devices, body(): lax.all_to_all(along_z, 'px', split_axis=2, concat_axis=3, tiled=True)  93.2 us
    all_to_all x1, waiting for transfers between devices, body(): lax.all_to_all(planes, 'px', split_axis=3, concat_axis=2, tiled=True)  78.7 us
    unnamed x18, local copies, waits for them, and re-layouts  56.6 us
    unnamed x3, other arithmetic  39.1 us
    all_to_all x1, blocking collectives, body(): lax.all_to_all(jnp.stack([back_real, back_imag], axis=0), 'py', split_axi...  28.9 us
    all_to_all x1, blocking collectives, body(): lax.all_to_all(along_x, 'py', split_axis=4, concat_axis=5, tiled=True)  28.9 us
  transfers between devices with their start and end apart: 3, of which 3 were waited for; matrix products, arithmetic and copies ran while one was open for 2% of the time, Pallas kernels for 0%

commit v1 on v0

--- a/solution.py
+++ b/solution.py
@@ -8,6 +8,17 @@
 MX = 64
 MY = 64
 MZ = 32
+
+
+def gather_by_hops(x, axis, dim):
+    size = lax.axis_size(axis)
+    right = [(i, (i + 1) % size) for i in range(size)]
+    terms = [x]
+    for far in range(1, size):
+        terms = [lax.ppermute(terms[0], axis, right), *terms]
+    out = jnp.concatenate(terms, axis=dim)
+    shift = (lax.axis_index(axis) + 1) * terms[-1].shape[dim]
+    return jnp.roll(out, shift, axis=dim)
 
 
 def contract(form, left, right):
@@ -71,7 +82,7 @@
         "bciky,yj->bcikj", moved[0], sin_y
     )
     spectrum = jnp.stack([spec_real, spec_imag], axis=0).astype(jnp.bfloat16)
-    gathered = lax.all_gather(spectrum, "px", axis=2, tiled=True)
+    gathered = gather_by_hops(spectrum, "px", 2)
     in_real = gathered[0].astype(jnp.float32)
     in_imag = gathered[1].astype(jnp.float32)
     weight_real = spectral_weight[0].astype(jnp.float32)

time: 756 us -> 829 us (1.097)
  waiting for transfers between devices: 295 us -> 343 us
  local copies, waits for them, and re-layouts: 139 us -> 168 us
  between operations: 14.2 us -> 0.59 us
    ppermute x0 -> x7, waiting for transfers between devices: none -> 172 us  [gather_by_hops(): terms = [lax.ppermute(terms[0], axis, right), *terms]]
    all_gather x1 -> x0, waiting for transfers between devices: 123 us -> none  [body(): gathered = lax.all_gather(spectrum, 'px', axis=2, tiled=True)]
    unnamed x18 -> x50, local copies, waits for them, and re-layouts: 56.6 us -> 86.6 us
    unnamed x3 -> x5, other arithmetic: 39.1 us -> 40.3 us
  transfers between devices with their start and end apart: 3 -> 9, of which waited for: 3 -> 9; matrix products, arithmetic and copies ran while one was open for 2% -> 2% of each run, Pallas kernels for 0% -> 0%
where the time goes in v1:
time: 829 us; the launch traced here: 818 us
  waiting for transfers between devices  343 us (41%)
  local copies, waits for them, and re-layouts  168 us (20%)
  matrix products  154 us (19%)
  other arithmetic  79.5 us (10%)
  blocking collectives  59 us (7%)
  starting transfers between devices  13.6 us (2%)
    ppermute x7, waiting for transfers between devices, gather_by_hops(): terms = [lax.ppermute(terms[0], axis, right), *terms]  172 us
    dot_general x19, matrix products, contract(): jnp.einsum(form, left, right, precision=lax.Precision.HIGHEST, preferred_...  140 us
    all_to_all x1, waiting for transfers between devices, body(): lax.all_to_all(along_z, 'px', split_axis=2, concat_axis=3, tiled=True)  93.3 us
    unnamed x50, local copies, waits for them, and re-layouts  86.6 us
    all_to_all x1, waiting for transfers between devices, body(): lax.all_to_all(planes, 'px', split_axis=3, concat_axis=2, tiled=True)  78.5 us
    unnamed x5, other arithmetic  40.3 us
    all_to_all x1, blocking collectives, body(): lax.all_to_all(jnp.stack([back_real, back_imag], axis=0), 'py', split_axi...  30.1 us
    all_to_all x1, blocking collectives, body(): lax.all_to_all(along_x, 'py', split_axis=4, concat_axis=5, tiled=True)  28.9 us
  transfers between devices with their start and end apart: 9, of which 9 were waited for; matrix products, arithmetic and copies ran while one was open for 2% of the time, Pallas kernels for 0%

profile of v1, /device:TPU:0, one launch (start us, length us, event | category | flops | bytes accessed | tf_op | source)
XLA Modules:
  0.0 818.4 jit_solution(16734713008782258587)
XLA Ops:
  0.0 24.2 %convolution_bitcast_fusion.1 = f32[1,32,16,32,32]{4,3,2,1,0:T(8,128)} fusion(bf16[1,32,16,32,256]{4,3,2,1,0:T(8,128)(2,1)} %param.4), kind=kOutput, calls=%fused_computation.41 | convolution fusion | flops 1610727424 | bytes 10485760 | tf_op jit(solution)/shard_map/bcxyz,zk->bcxky/dot_general | solution.py:25
  24.2 21.1 %convolution_bitcast_fusion = f32[1,32,16,32,32]{4,3,2,1,0:T(8,128)} fusion(bf16[1,32,16,32,256]{4,3,2,1,0:T(8,128)(2,1)S(1)} %copy-done.2), kind=kOutput, calls=%fused_computation.40 | convolution fusion | flops 1610735616 | bytes 10485760 | tf_op jit(solution)/shard_map/bcxyz,zk->bcxky/dot_general | solution.py:25
  45.4 6.6 stack.50
  52.0 8.2 stack.51
  60.2 4.4 pad_maximum_fusion
  64.6 7.3 all-to-all-start
  71.9 93.3 %all-to-all-done = f32[2,1,32,16,1024]{4,3,1,0,2:T(8,128)} async-done(((f32[2,1,32,16,1024]{4,3,1,0,2:T(8,128)}), f32[2,1,32,16,1024]{4,3,1,0,2:T(8,128)}, u32[]{:S(2)}, u32[]{:S(2)}) %all-to-all-start) | async-done | bytes 4194336 | tf_op jit(solution)/shard_map/all_to_all | solution.py:72
  165.2 2.5 copy.147
  169.8 2.5 fusion.63
  175.8 2.9 fusion.20
  179.3 4.4 copy_bitcast_fusion.2
  183.7 4.5 reshape.325
  188.2 28.9 %all_to_all.60 = f32[4,1,131072]{2,1,0:T(1,128)} all-to-all(f32[4,1,131072]{2,1,0:T(1,128)S(1)} %reshape.325), channel_id=1, replica_groups=mesh['px'=8,'py'=4] {'py'}, dimensions={0} | all-to-all | bytes 4194304 | tf_op jit(solution)/shard_map/all_to_all | solution.py:75
  217.6 7.6 reduce.8
  225.2 4.0 reshape.326
  229.2 2.8 copy.146
  232.1 2.0 fusion.178
  234.7 2.1 fusion.59
  236.8 2.2 copy.55
  240.3 2.8 fusion.25
  246.0 25.8 %collective-permute-done = bf16[2,1,4,64,8,64]{5,4,3,2,1,0:T(8,128)(2,1)S(1)} collective-permute-done((bf16[2,1,4,64,8,64]{5,4,3,2,1,0:T(8,128)(2,1)S(1)}, bf16[2,1,4,64,8,64]{5,4,3,2,1,0:T(8,128)(2,1)S(1)}, u32[]{:S(2)}, u32[]{:S(2)}) %collective-permute-start) | collective-permute-done | bytes 524320 | tf_op jit(solution)/shard_map/ppermute | solution.py:18
  271.8 26.4 %collective-permute-done.1 = bf16[2,1,4,64,8,64]{5,4,3,2,1,0:T(8,128)(2,1)S(1)} collective-permute-done((bf16[2,1,4,64,8,64]{5,4,3,2,1,0:T(8,128)(2,1)S(1)}, bf16[2,1,4,64,8,64]{5,4,3,2,1,0:T(8,128)(2,1)S(1)}, u32[]{:S(2)}, u32[]{:S(2)}) %collective-permute-start.1) | collective-permute-done | bytes 524320 | tf_op jit(solution)/shard_map/ppermute | solution.py:18
  299.1 25.5 %collective-permute-done.2 = bf16[2,1,4,64,8,64]{5,4,3,2,1,0:T(8,128)(2,1)S(1)} collective-permute-done((bf16[2,1,4,64,8,64]{5,4,3,2,1,0:T(8,128)(2,1)S(1)}, bf16[2,1,4,64,8,64]{5,4,3,2,1,0:T(8,128)(2,1)S(1)}, u32[]{:S(2)}, u32[]{:S(2)}) %collective-permute-start.2) | collective-permute-done | bytes 524320 | tf_op jit(solution)/shard_map/ppermute | solution.py:18
  325.7 24.7 %collective-permute-done.3 = bf16[2,1,4,64,8,64]{5,4,3,2,1,0:T(8,128)(2,1)S(1)} collective-permute-done((bf16[2,1,4,64,8,64]{5,4,3,2,1,0:T(8,128)(2,1)S(1)}, bf16[2,1,4,64,8,64]{5,4,3,2,1,0:T(8,128)(2,1)S(1)}, u32[]{:S(2)}, u32[]{:S(2)}) %collective-permute-start.3) | collective-permute-done | bytes 524320 | tf_op jit(solution)/shard_map/ppermute | solution.py:18
  351.3 23.8 %collective-permute-done.4 = bf16[2,1,4,64,8,64]{5,4,3,2,1,0:T(8,128)(2,1)S(1)} collective-permute-done((bf16[2,1,4,64,8,64]{5,4,3,2,1,0:T(8,128)(2,1)S(1)}, bf16[2,1,4,64,8,64]{5,4,3,2,1,0:T(8,128)(2,1)S(1)}, u32[]{:S(2)}, u32[]{:S(2)}) %collective-permute-start.4) | collective-permute-done | bytes 524320 | tf_op jit(solution)/shard_map/ppermute | solution.py:18
  376.1 23.1 %collective-permute-done.5 = bf16[2,1,4,64,8,64]{5,4,3,2,1,0:T(8,128)(2,1)} collective-permute-done((bf16[2,1,4,64,8,64]{5,4,3,2,1,0:T(8,128)(2,1)S(1)}, bf16[2,1,4,64,8,64]{5,4,3,2,1,0:T(8,128)(2,1)}, u32[]{:S(2)}, u32[]{:S(2)}) %collective-permute-start.5) | collective-permute-done | bytes 524320 | tf_op jit(solution)/shard_map/ppermute | solution.py:18
  399.2 22.4 %collective-permute-done.6 = bf16[2,1,4,64,8,64]{5,4,3,2,1,0:T(8,128)(2,1)} collective-permute-done((bf16[2,1,4,64,8,64]{5,4,3,2,1,0:T(8,128)(2,1)}, bf16[2,1,4,64,8,64]{5,4,3,2,1,0:T(8,128)(2,1)}, u32[]{:S(2)}, u32[]{:S(2)}) %collective-permute-start.6) | collective-permute-done | bytes 524320 | tf_op jit(solution)/shard_map/ppermute | solution.py:18
  421.6 2.4 constant_dynamic-update-slice_fusion.15
  424.0 2.4 constant_dynamic-update-slice_fusion.14
  426.4 2.4 constant_dynamic-update-slice_fusion.13
  428.8 2.4 constant_dynamic-update-slice_fusion.12
  431.1 2.4 constant_dynamic-update-slice_fusion.11
  433.5 2.4 constant_dynamic-update-slice_fusion.10
  438.2 2.4 constant_dynamic-update-slice_fusion.7
  440.6 2.4 constant_dynamic-update-slice_fusion.6
  450.0 11.6 %fusion.16 = (f32[64,8,64,32]{2,1,0,3:T(8,128)}, f32[64,8,64,32]{2,1,0,3:T(8,128)}) fusion(bf16[2,1,64,64,8,64]{5,4,3,2,1,0:T(8,128)(2,1)} %constant_dynamic-update-slice_fusion, s32[]{:T(128)S(6)} %add.156, s32[]{:T(128)S(6)} %select_n.133), kind=kLoop, calls=%fused_computation.32 | loop fusion | flops 2097152 | bytes 12582920
  461.6 8.4 %copy.106 = f32[64,8,64,32]{2,0,1,3:T(8,128)} copy(f32[64,8,64,32]{2,1,0,3:T(8,128)} %get-tuple-element.12) | data formatting | bytes 8388608
  470.0 5.0 copy.107
  475.0 23.1 %fusion.3 = (f32[64,8,64,4]{2,0,1,3:T(8,128)S(1)}, f32[64,8,64,4]{2,0,1,3:T(8,128)S(1)}, f32[64,8,64,4]{2,0,1,3:T(8,128)}, f32[64,8,64,4]{2,0,1,3:T(8,128)S(1)}) fusion(f32[64,8,64,32]{2,0,1,3:T(8,128)} %copy.106, bf16[2,32,4,8,64,64]{5,4,3,2,1,0:T(8,128)(2,1)} %param.5, f32[64,8,64,32]{2,0,1,3:T(8,128)} %copy.107), kind=kLoop, calls=%fused_computation.7 | loop fusion | flops 41418752 | bytes 27262976
  498.2 3.8 fusion.30
  502.0 3.8 fusion.28
  505.8 2.4 fusion.19
  508.2 2.4 fusion.18
  510.7 4.7 copy.58
  515.4 4.5 reshape.327
  519.9 30.1 %all_to_all.61 = f32[4,1,131072]{2,1,0:T(1,128)} all-to-all(f32[4,1,131072]{2,1,0:T(1,128)S(1)} %reshape.327), channel_id=1, replica_groups=mesh['px'=8,'py'=4] {'py'}, dimensions={0} | all-to-all | bytes 4194304 | tf_op jit(solution)/shard_map/all_to_all | solution.py:104
  550.0 7.6 reduce.9
  557.6 4.0 reshape.328
  561.6 4.6 copy.59
  567.3 2.5 fusion.53
  569.7 2.1 fusion.45
  572.0 2.0 subtract_bitcast_fusion
  574.1 2.0 add_bitcast_fusion
  576.1 2.8 pad_maximum_fusion.2
  578.9 14.4 %copy.62 = f32[2,1,4,128,32,32]{5,4,2,1,0,3:T(8,128)} copy(f32[2,1,4,128,32,32]{3,5,4,2,1,0:T(8,128)} %pad_maximum_fusion.2) | data formatting | bytes 8388608 | tf_op jit(solution)/shard_map/stack | solution.py:115
  593.3 12.8 %reshape.329 = f32[8,1,131072]{2,1,0:T(1,128)} reshape(f32[128,2,1,4,32,32]{5,4,3,2,1,0:T(8,128)} %bitcast.215) | data formatting | bytes 8388608
  606.1 4.7 all-to-all-start.3
  611.2 14.2 %fusion.14 = f32[16,32,256,32]{2,3,1,0:T(8,128)} fusion(bf16[32,16,32,256]{3,2,1,0:T(8,128)(2,1)} %bitcast.214, bf16[32,32]{1,0:T(8,128)(2,1)S(1)} %copy-done), kind=kOutput, calls=%fused_computation.29 | convolution fusion | flops 268435456 | bytes 25167872 | tf_op jit(solution)/shard_map/oc,bcxyz->boxyz/dot_general | solution.py:126
  625.4 78.5 %all-to-all-done.3 = f32[8,1,131072]{2,1,0:T(1,128)} async-done(((f32[8,1,131072]{2,1,0:T(1,128)}), f32[8,1,131072]{2,1,0:T(1,128)}, u32[]{:S(2)}, u32[]{:S(2)}) %all-to-all-start.3) | async-done | bytes 4194336 | tf_op jit(solution)/shard_map/all_to_all | solution.py:124
  703.9 14.9 %reduce.10 = f32[8,131072]{1,0:T(8,128)} reduce(f32[8,1,131072]{2,1,0:T(1,128)} %all-to-all-done.3, f32[]{:T(128)} %broadcast.332), dimensions={1}, to_apply=%all_to_all.53.reduce_sub_computation | reduce | bytes 8388612 | tf_op jit(solution)/shard_map/all_to_all | solution.py:124
  718.8 13.3 %reshape.330 = f32[128,2,1,4,32,32]{5,4,3,2,1,0:T(8,128)} reshape(f32[8,131072]{1,0:T(8,128)} %reduce.10) | data formatting | bytes 8388608
  732.1 11.8 %copy.63 = f32[2,1,4,128,32,32]{5,4,3,2,0,1:T(8,128)} copy(f32[2,1,4,128,32,32]{5,4,2,1,0,3:T(8,128)} %bitcast.216) | data formatting | bytes 8388608 | tf_op jit(solution)/shard_map/all_to_all | solution.py:124
  743.9 16.5 %copy.64 = f32[2,1,8,4,16,32,32]{5,6,0,4,3,2,1:T(8,128)} copy(f32[2,1,8,4,16,32,32]{6,5,4,2,3,0,1:T(8,128)} %bitcast.217) | data formatting | bytes 8388608 | tf_op jit(solution)/shard_map/all_to_all | solution.py:124
  760.4 57.7 %fusion.6 = bf16[1,32,16,32,256]{4,3,2,1,0:T(8,128)(2,1)} fusion(f32[16,32,256,32]{2,3,1,0:T(8,128)} %fusion.14, f32[2,32,16,32,32]{3,4,0,2,1:T(8,128)} %bitcast.229, f32[32]{0:T(128)S(1)} %copy-done.11, f32[1,32,256]{2,1,0:T(8,128)S(1)} %sine_multiply_fusion, f32[1,32,256]{2,1,0:T(8,128)S(1)} %cosine_multiply_fusion), kind=kOutput, calls=%fused_computation.11 | convolution fusion | flops 3502260224 | bytes 29425792 | tf_op jit(solution)/shard_map/pbcxky,pkz->bcxyz/dot_general | solution.py:25
  (62 shorter events, 26.4 us)
Async XLA Ops:
  0.0 611.1 %copy-start = (bf16[32,32]{1,0:T(8,128)(2,1)S(1)}, bf16[32,32]{1,0:T(8,128)(2,1)}, u32[]{:S(2)}) copy-start(bf16[32,32]{1,0:T(8,128)(2,1)} %param.6) | copy-start | bytes 6148
  0.0 24.2 %copy-start.2 = (bf16[1,32,16,32,256]{4,3,2,1,0:T(8,128)(2,1)S(1)}, bf16[1,32,16,32,256]{4,3,2,1,0:T(8,128)(2,1)}, u32[]{:S(2)}) copy-start(bf16[1,32,16,32,256]{4,3,2,1,0:T(8,128)(2,1)} %param.4) | copy-start | bytes 25165828
  64.6 100.6 %all-to-all-start = ((f32[2,1,32,16,1024]{4,3,1,0,2:T(8,128)}), f32[2,1,32,16,1024]{4,3,1,0,2:T(8,128)}, u32[]{:S(2)}, u32[]{:S(2)}) async-start(f32[2,1,32,16,1024]{4,3,1,0,2:T(8,128)} %pad_maximum_fusion), calls=%async_computation | async-start | bytes 8388608 | tf_op jit(solution)/shard_map/all_to_all | solution.py:72
  244.5 27.3 %collective-permute-start = (bf16[2,1,4,64,8,64]{5,4,3,2,1,0:T(8,128)(2,1)S(1)}, bf16[2,1,4,64,8,64]{5,4,3,2,1,0:T(8,128)(2,1)S(1)}, u32[]{:S(2)}, u32[]{:S(2)}) collective-permute-start(bf16[2,1,4,64,8,64]{5,4,3,2,1,0:T(8,128)(2,1)S(1)} %pad_maximum_fusion.4), channel_id=1, source_target_pairs={{0,4},{4,8},{8,12},{12,16},{16,20},{20,24},{24,28},{28,0},{1,5},{5... | collective-permute-start | bytes 1572872 | tf_op jit(solution)/shard_map/ppermute | solution.py:18
  271.8 26.4 %collective-permute-start.1 = (bf16[2,1,4,64,8,64]{5,4,3,2,1,0:T(8,128)(2,1)S(1)}, bf16[2,1,4,64,8,64]{5,4,3,2,1,0:T(8,128)(2,1)S(1)}, u32[]{:S(2)}, u32[]{:S(2)}) collective-permute-start(bf16[2,1,4,64,8,64]{5,4,3,2,1,0:T(8,128)(2,1)S(1)} %collective-permute-done), channel_id=1, source_target_pairs={{0,4},{4,8},{8,12},{12,16},{16,20},{20,24},{24,28},{28,0},{1,5},{5... | collective-permute-start | bytes 1572872 | tf_op jit(solution)/shard_map/ppermute | solution.py:18
  298.1 1.0 copy-start.3
  299.1 25.5 %collective-permute-start.2 = (bf16[2,1,4,64,8,64]{5,4,3,2,1,0:T(8,128)(2,1)S(1)}, bf16[2,1,4,64,8,64]{5,4,3,2,1,0:T(8,128)(2,1)S(1)}, u32[]{:S(2)}, u32[]{:S(2)}) collective-permute-start(bf16[2,1,4,64,8,64]{5,4,3,2,1,0:T(8,128)(2,1)S(1)} %collective-permute-done.1), channel_id=1, source_target_pairs={{0,4},{4,8},{8,12},{12,16},{16,20},{20,24},{24,28},{28,0},{1,5},{5... | collective-permute-start | bytes 1572872 | tf_op jit(solution)/shard_map/ppermute | solution.py:18
  324.7 1.0 copy-start.5
  325.7 24.7 %collective-permute-start.3 = (bf16[2,1,4,64,8,64]{5,4,3,2,1,0:T(8,128)(2,1)S(1)}, bf16[2,1,4,64,8,64]{5,4,3,2,1,0:T(8,128)(2,1)S(1)}, u32[]{:S(2)}, u32[]{:S(2)}) collective-permute-start(bf16[2,1,4,64,8,64]{5,4,3,2,1,0:T(8,128)(2,1)S(1)} %collective-permute-done.2), channel_id=1, source_target_pairs={{0,4},{4,8},{8,12},{12,16},{16,20},{20,24},{24,28},{28,0},{1,5},{5... | collective-permute-start | bytes 1572872 | tf_op jit(solution)/shard_map/ppermute | solution.py:18
  350.3 1.0 copy-start.7
  351.3 23.8 %collective-permute-start.4 = (bf16[2,1,4,64,8,64]{5,4,3,2,1,0:T(8,128)(2,1)S(1)}, bf16[2,1,4,64,8,64]{5,4,3,2,1,0:T(8,128)(2,1)S(1)}, u32[]{:S(2)}, u32[]{:S(2)}) collective-permute-start(bf16[2,1,4,64,8,64]{5,4,3,2,1,0:T(8,128)(2,1)S(1)} %collective-permute-done.3), channel_id=1, source_target_pairs={{0,4},{4,8},{8,12},{12,16},{16,20},{20,24},{24,28},{28,0},{1,5},{5... | collective-permute-start | bytes 1572872 | tf_op jit(solution)/shard_map/ppermute | solution.py:18
  375.1 1.0 copy-start.9
  376.1 23.1 %collective-permute-start.5 = (bf16[2,1,4,64,8,64]{5,4,3,2,1,0:T(8,128)(2,1)S(1)}, bf16[2,1,4,64,8,64]{5,4,3,2,1,0:T(8,128)(2,1)}, u32[]{:S(2)}, u32[]{:S(2)}) collective-permute-start(bf16[2,1,4,64,8,64]{5,4,3,2,1,0:T(8,128)(2,1)S(1)} %collective-permute-done.4), channel_id=1, source_target_pairs={{0,4},{4,8},{8,12},{12,16},{16,20},{20,24},{24,28},{28,0},{1,5},{5... | collective-permute-start | bytes 1572872 | tf_op jit(solution)/shard_map/ppermute | solution.py:18
  399.2 22.4 %collective-permute-start.6 = (bf16[2,1,4,64,8,64]{5,4,3,2,1,0:T(8,128)(2,1)}, bf16[2,1,4,64,8,64]{5,4,3,2,1,0:T(8,128)(2,1)}, u32[]{:S(2)}, u32[]{:S(2)}) collective-permute-start(bf16[2,1,4,64,8,64]{5,4,3,2,1,0:T(8,128)(2,1)} %collective-permute-done.5), channel_id=1, source_target_pairs={{0,4},{4,8},{8,12},{12,16},{16,20},{20,24},{24,28},{28,0},{1,5},{5... | collective-permute-start | bytes 1572872 | tf_op jit(solution)/shard_map/ppermute | solution.py:18
  399.2 43.8 %copy-start.10 = (bf16[2,1,4,64,8,64]{5,4,3,2,1,0:T(8,128)(2,1)S(1)}, bf16[2,1,4,64,8,64]{5,4,3,2,1,0:T(8,128)(2,1)}, u32[]{:S(2)}) copy-start(bf16[2,1,4,64,8,64]{5,4,3,2,1,0:T(8,128)(2,1)} %copy-done.9) | copy-start | bytes 1572868
  399.2 45.0 %copy-start.8 = (bf16[2,1,4,64,8,64]{5,4,3,2,1,0:T(8,128)(2,1)S(1)}, bf16[2,1,4,64,8,64]{5,4,3,2,1,0:T(8,128)(2,1)}, u32[]{:S(2)}) copy-start(bf16[2,1,4,64,8,64]{5,4,3,2,1,0:T(8,128)(2,1)} %copy-done.7) | copy-start | bytes 1572868
  399.2 46.1 %copy-start.6 = (bf16[2,1,4,64,8,64]{5,4,3,2,1,0:T(8,128)(2,1)S(1)}, bf16[2,1,4,64,8,64]{5,4,3,2,1,0:T(8,128)(2,1)}, u32[]{:S(2)}) copy-start(bf16[2,1,4,64,8,64]{5,4,3,2,1,0:T(8,128)(2,1)} %copy-done.5) | copy-start | bytes 1572868
  399.2 47.3 %copy-start.4 = (bf16[2,1,4,64,8,64]{5,4,3,2,1,0:T(8,128)(2,1)S(1)}, bf16[2,1,4,64,8,64]{5,4,3,2,1,0:T(8,128)(2,1)}, u32[]{:S(2)}) copy-start(bf16[2,1,4,64,8,64]{5,4,3,2,1,0:T(8,128)(2,1)} %copy-done.3) | copy-start | bytes 1572868
  461.6 8.4 %slice-start = ((s8[8388608]{0:T(1024)(128)(4,1)}), s8[4194304]{0:T(1024)(128)(4,1)S(1)}, s32[]{:S(2)}) async-start(s8[8388608]{0:T(1024)(128)(4,1)} %bitcast.218), calls=%async_computation.4 | async-start | bytes 8388608
  461.6 8.4 %slice-start.1 = ((s8[8388608]{0:T(1024)(128)(4,1)}), s8[4194304]{0:T(1024)(128)(4,1)S(1)}, s32[]{:S(2)}) async-start(s8[8388608]{0:T(1024)(128)(4,1)} %bitcast.218), calls=%async_computation.5 | async-start | bytes 8388608
  606.1 97.8 %all-to-all-start.3 = ((f32[8,1,131072]{2,1,0:T(1,128)}), f32[8,1,131072]{2,1,0:T(1,128)}, u32[]{:S(2)}, u32[]{:S(2)}) async-start(f32[8,1,131072]{2,1,0:T(1,128)} %reshape.329), calls=%async_computation.3 | async-start | bytes 8388608 | tf_op jit(solution)/shard_map/all_to_all | solution.py:124
  743.9 16.5 %copy-start.11 = (f32[32]{0:T(128)S(1)}, f32[32]{0:T(128)}, u32[]{:S(2)}) copy-start(f32[32]{0:T(128)} %param.7) | copy-start | bytes 388
  760.4 57.7 %copy-start.1 = (bf16[32,32]{1,0:T(8,128)(2,1)S(1)}, bf16[32,32]{1,0:T(8,128)(2,1)}, u32[]{:S(2)}) copy-start(bf16[32,32]{1,0:T(8,128)(2,1)} %param.6) | copy-start | bytes 6148
